TPU v7x, 8 devices: a whole 2x2x1 slice. The times are simulated.
8 devices in a mesh: batch: 2 (over z, y), time: 4 (over x, core).
Axes of the slice: x: 2, y: 2, z: 1, core: 2. Of those that a mesh axis runs over, the one named last changes fastest.
Arguments:
- latent: bfloat16 [16, 4, 96, 768], P(('batch', 'time')), parts along dimension 0
- conv_w: bfloat16 [4, 3, 3, 3, 768, 768], replicated
- conv_b: float32 [4, 768], replicated
- norm_g: float32 [5, 768], replicated
- norm_b: float32 [5, 768], replicated
- attn_w: bfloat16 [4, 768, 768], replicated
- attn_b: float32 [4, 768], replicated
Outputs:
- output: bfloat16 [16, 4, 96, 768], P(('batch', 'time')), parts along dimension 0
There are 2 independent parts. A program takes and returns all parts, laid end to end along the dimension named above; an argument that names none is the same for every part.
All inputs are finite; a program needn't handle non-finite values.
Results may differ from a plain program's by a relative error of at most 0.0124034.
Values are sent between devices in bfloat16 or wider.
A program may use at most 1 GiB of HBM per device.

v0:
```python
import jax
import jax.numpy as jnp
from jax import lax
from jax.sharding import PartitionSpec as P

GROUPS = 32
NORM_EPS = 1e-6


def group_stats(feature):
    channels = feature.shape[-1]
    grouped = feature.reshape(feature.shape[:-1] + (GROUPS, channels // GROUPS)).astype(jnp.float32)
    return jnp.stack([jnp.sum(grouped, axis=(0, 1, 2, 4)), jnp.sum(grouped * grouped, axis=(0, 1, 2, 4))])


def apply_norm(feature, totals, elem_count, norm_gain, norm_shift):
    channels = feature.shape[-1]
    group_mean = totals[0] / elem_count
    inv_std = lax.rsqrt(totals[1] / elem_count - group_mean * group_mean + NORM_EPS)
    mean_full = jnp.repeat(group_mean, channels // GROUPS)
    scale_full = jnp.repeat(inv_std, channels // GROUPS) * norm_gain
    return (feature.astype(jnp.float32) - mean_full) * scale_full + norm_shift


def halo_conv(activation, kernel, conv_bias, group_size):
    prev_frames = lax.ppermute(activation[-2:], "time", [(source, source + 1) for source in range(group_size - 1)])
    first_copy = jnp.broadcast_to(activation[:1], prev_frames.shape)
    prev_frames = jnp.where(lax.axis_index("time") == 0, first_copy, prev_frames)
    padded = jnp.concatenate([prev_frames, activation], axis=0)
    conv_out = lax.conv_general_dilated(padded[None], kernel, (1, 1, 1), ((0, 0), (1, 1), (1, 1)), dimension_numbers=("NDHWC", "DHWIO", "NDHWC"), preferred_element_type=jnp.float32)
    return (conv_out[0] + conv_bias).astype(jnp.bfloat16)


def frame_attention(normed, attn_w, attn_b):
    frames, img_height, img_width, channels = normed.shape
    tokens = normed.reshape(frames, img_height * img_width, channels)
    proj_in = jnp.einsum("fsc,kcd->kfsd", tokens, attn_w[:3], preferred_element_type=jnp.float32)
    proj_in = (proj_in + attn_b[:3, None, None, :]).astype(jnp.bfloat16)
    scores = jnp.einsum("fsd,ftd->fst", proj_in[0], proj_in[1], preferred_element_type=jnp.float32) * channels ** -0.5
    attn_probs = jax.nn.softmax(scores, axis=-1).astype(jnp.bfloat16)
    mixed_val = jnp.einsum("fst,ftd->fsd", attn_probs, proj_in[2], preferred_element_type=jnp.float32).astype(jnp.bfloat16)
    out_proj = jnp.einsum("fsd,de->fse", mixed_val, attn_w[3], preferred_element_type=jnp.float32) + attn_b[3]
    return out_proj.astype(jnp.bfloat16).reshape(normed.shape)


def solution(mesh):
    group_size = mesh.shape["time"]
    video_spec = P(("batch", "time"), None, None, None)

    def device_body(latent, conv_w, conv_b, norm_g, norm_b, attn_w, attn_b):
        frames_dev, img_height, img_width, channels = latent.shape
        elem_count = group_size * frames_dev * img_height * img_width * (channels // GROUPS)

        def norm_full(feature, norm_index):
            totals = lax.psum(group_stats(feature), "time")
            return apply_norm(feature, totals, elem_count, norm_g[norm_index], norm_b[norm_index])

        def resnet_block(feature, norm_first, conv_first):
            activation = jax.nn.silu(norm_full(feature, norm_first)).astype(jnp.bfloat16)
            branch = halo_conv(activation, conv_w[conv_first], conv_b[conv_first], group_size)
            activation = jax.nn.silu(norm_full(branch, norm_first + 1)).astype(jnp.bfloat16)
            branch = halo_conv(activation, conv_w[conv_first + 1], conv_b[conv_first + 1], group_size)
            return feature + branch

        feature = resnet_block(latent, 0, 0)
        normed = norm_full(feature, 2).astype(jnp.bfloat16)
        feature = feature + frame_attention(normed, attn_w, attn_b)
        return resnet_block(feature, 3, 2)

    return jax.shard_map(device_body, mesh=mesh, in_specs=(video_spec, P(), P(), P(), P(), P(), P()), out_specs=video_spec, check_vma=False)
```

profile of v0, /device:TPU:6, one launch (start us, length us, event | category | flops | bytes accessed | tf_op | source)
XLA Modules:
  0.0 283.2 jit_solution(14780532954171973947)
XLA Ops:
  2.1 5.9 %psum.35 = f32[2,32]{1,0:T(2,128)S(1)} all-reduce(f32[2,32]{1,0:T(2,128)S(1)} %pad_maximum_fusion), channel_id=1, replica_groups=mesh['batch'=2,'time'=4] {'time'}, use_global_device_ids=true, to_apply=%region_4.5 | all-reduce | flops 64 | bytes 512 | tf_op jit(solution)/shard_map/psum | solution.py:55
  10.8 2.0 fusion.59
  12.9 1.9 collective-permute-start
  15.5 14.9 %collective-permute-done = bf16[2,4,96,768]{3,2,1,0:T(8,128)(2,1)S(1)} collective-permute-done((bf16[2,4,96,768]{3,2,1,0:T(8,128)(2,1)S(1)}, bf16[2,4,96,768]{3,2,1,0:T(8,128)(2,1)S(1)}, u32[]{:S(2)}, u32[]{:S(2)}) %collective-permute-start) | collective-permute-done | bytes 1179680 | tf_op jit(solution)/shard_map/ppermute | solution.py:26
  30.7 1.8 copy.69
  34.2 32.5 %fusion.45 = (f32[768]{0:T(1024)S(1)}, f32[768]{0:T(1024)S(1)}, f32[2,4,8,13,768]{4,2,3,1,0:T(8,128)S(1)}) fusion(pred[8,13]{0,1:T(8,128)(4,1)S(1)} %copy-done.6, f32[768]{0:T(1024)S(1)} %get-tuple-element.27, bf16[4,3,3,3,768,768]{5,4,3,2,1,0:T(8,128)(2,1)} %param.8, bf16[4,4,1,7,2,768]{5,3,4,1,0,2:T(8,128)(2,1)S(1)} %slice.165, ...), kind=kOutput, calls=%fused_computation.56 | convolution fusion | flops 22097608704 | bytes 37315688 | tf_op jit(solution)/shard_map/conv_general_dilated | solution.py:30
  67.1 5.8 %psum.36 = f32[2,32]{1,0:T(2,128)S(1)} all-reduce(f32[2,32]{1,0:T(2,128)S(1)} %pad_maximum_fusion.1), channel_id=1, replica_groups=mesh['batch'=2,'time'=4] {'time'}, use_global_device_ids=true, to_apply=%region_9.10 | all-reduce | flops 64 | bytes 512 | tf_op jit(solution)/shard_map/psum | solution.py:55
  75.5 2.1 collective-permute-start.1
  78.3 14.8 %collective-permute-done.1 = bf16[2,4,96,768]{3,2,1,0:T(8,128)(2,1)S(1)} collective-permute-done((bf16[2,4,96,768]{3,2,1,0:T(8,128)(2,1)S(1)}, bf16[2,4,96,768]{3,2,1,0:T(8,128)(2,1)S(1)}, u32[]{:S(2)}, u32[]{:S(2)}) %collective-permute-start.1) | collective-permute-done | bytes 1179680 | tf_op jit(solution)/shard_map/ppermute | solution.py:26
  93.4 1.8 copy.70
  96.6 31.5 %fusion.93 = f32[2,4,8,13,768]{4,2,3,1,0:T(8,128)S(1)} fusion(bf16[4,3,3,3,768,768]{5,4,3,2,1,0:T(8,128)(2,1)} %param.8, bf16[4,4,1,7,2,768]{5,3,4,1,0,2:T(8,128)(2,1)S(1)} %slice.168, bf16[4,4,1,8,13,768]{5,3,4,1,0,2:T(8,128)(2,1)S(1)} %copy.49, pred[8,13]{0,1:T(8,128)(4,1)S(1)} %copy-done.6), kind=kOutput, calls=%fused_computation.112 | convolution fusion | flops 22092496896 | bytes 37306472 | tf_op jit(solution)/shard_map/conv_general_dilated | solution.py:30
  131.4 6.0 %psum.37 = f32[2,32]{1,0:T(2,128)S(1)} all-reduce(f32[2,32]{1,0:T(2,128)S(1)} %pad_maximum_fusion.2), channel_id=1, replica_groups=mesh['batch'=2,'time'=4] {'time'}, use_global_device_ids=true, to_apply=%region_14.15 | all-reduce | flops 64 | bytes 512 | tf_op jit(solution)/shard_map/psum | solution.py:55
  138.1 5.2 %fusion.17 = bf16[3,2,384,768]{3,2,0,1:T(8,128)(2,1)S(1)} fusion(f32[3,768]{1,0:T(4,128)S(1)} %bitcast.217, bf16[2,384,768,1]{2,1,3,0:T(8,128)(2,1)S(1)} %bitcast.206, bf16[4,768,768]{2,1,0:T(8,128)(2,1)} %param.12), kind=kOutput, calls=%fused_computation.19 | convolution fusion | flops 2721447936 | bytes 8266752 | tf_op jit(solution)/shard_map/fsc,kcd->kfsd/dot_general | solution.py:37
  145.9 3.6 %add_convert_fusion.3 = bf16[2,384,768]{2,1,0:T(8,128)(2,1)S(1)} fusion(f32[768]{0:T(1024)S(1)} %copy-done.4, bf16[4,768,768]{2,1,0:T(8,128)(2,1)} %param.12, bf16[3,2,384,768]{3,2,0,1:T(8,128)(2,1)} %copy-done.8, f32[2,384]{1,0:T(2,128)} %fusion.140, f32[2,384,384]{1,2,0:T(8,128)S(1)} %convolution_multiply_fusion), kind=kOutput, calls=%fused_computation.103 | convolution fusion | flops 1361609856 | bytes 5905408 | tf_op jit(solution)/shard_map/fsd,de->fse/dot_general | solution.py:42
  151.7 5.8 %psum.38 = f32[2,32]{1,0:T(2,128)S(1)} all-reduce(f32[2,32]{1,0:T(2,128)S(1)} %pad_maximum_fusion.3), channel_id=1, replica_groups=mesh['batch'=2,'time'=4] {'time'}, use_global_device_ids=true, to_apply=%region_21.22 | all-reduce | flops 64 | bytes 512 | tf_op jit(solution)/shard_map/psum | solution.py:55
  159.3 1.9 collective-permute-start.2
  161.2 15.5 %collective-permute-done.2 = bf16[2,4,96,768]{3,2,1,0:T(8,128)(2,1)S(1)} collective-permute-done((bf16[2,4,96,768]{3,2,1,0:T(8,128)(2,1)S(1)}, bf16[2,4,96,768]{3,2,1,0:T(8,128)(2,1)S(1)}, u32[]{:S(2)}, u32[]{:S(2)}) %collective-permute-start.2) | collective-permute-done | bytes 1179680 | tf_op jit(solution)/shard_map/ppermute | solution.py:26
  180.6 32.7 %fusion.48 = (f32[768]{0:T(1024)S(1)}, f32[768]{0:T(1024)S(1)}, f32[2,4,8,13,768]{4,2,3,1,0:T(8,128)}) fusion(pred[8,13]{0,1:T(8,128)(4,1)S(1)} %copy-done.7, f32[768]{0:T(1024)S(1)} %get-tuple-element.28, bf16[4,3,3,3,768,768]{5,4,3,2,1,0:T(8,128)(2,1)} %param.8, bf16[4,4,1,7,2,768]{5,3,4,1,0,2:T(8,128)(2,1)S(1)} %slice.174, ...), kind=kOutput, calls=%fused_computation.59 | convolution fusion | flops 22097608704 | bytes 37315688 | tf_op jit(solution)/shard_map/conv_general_dilated | solution.py:30
  213.7 5.9 %psum.39 = f32[2,32]{1,0:T(2,128)S(1)} all-reduce(f32[2,32]{1,0:T(2,128)S(1)} %pad_maximum_fusion.4), channel_id=1, replica_groups=mesh['batch'=2,'time'=4] {'time'}, use_global_device_ids=true, to_apply=%region_26.27 | all-reduce | flops 64 | bytes 512 | tf_op jit(solution)/shard_map/psum | solution.py:55
  220.0 2.7 copy.56
  224.2 1.9 collective-permute-start.3
  226.2 15.5 %collective-permute-done.3 = bf16[2,4,96,768]{3,2,1,0:T(8,128)(2,1)S(1)} collective-permute-done((bf16[2,4,96,768]{3,2,1,0:T(8,128)(2,1)S(1)}, bf16[2,4,96,768]{3,2,1,0:T(8,128)(2,1)S(1)}, u32[]{:S(2)}, u32[]{:S(2)}) %collective-permute-start.3) | collective-permute-done | bytes 1179680 | tf_op jit(solution)/shard_map/ppermute | solution.py:26
  245.3 32.7 %fusion.103 = f32[2,4,8,13,768]{4,2,3,1,0:T(8,128)} fusion(bf16[4,3,3,3,768,768]{5,4,3,2,1,0:T(8,128)(2,1)} %param.8, bf16[4,4,1,7,2,768]{5,3,4,1,0,2:T(8,128)(2,1)S(1)} %slice.177, bf16[4,4,1,8,13,768]{5,3,4,1,0,2:T(8,128)(2,1)S(1)} %copy.60, pred[8,13]{0,1:T(8,128)(4,1)S(1)} %copy-done.7), kind=kOutput, calls=%fused_computation.114 | convolution fusion | flops 22092496896 | bytes 37306472 | tf_op jit(solution)/shard_map/conv_general_dilated | solution.py:30
  278.0 2.7 copy.61
  (124 shorter events, 35.1 us)
Async XLA Ops:
  0.0 14.8 %copy-start.3 = (f32[4,768]{1,0:T(4,128)S(1)}, f32[4,768]{1,0:T(4,128)}, u32[]{:S(2)}) copy-start(f32[4,768]{1,0:T(4,128)} %param.9) | copy-start | bytes 36868
  12.9 17.5 %collective-permute-start = (bf16[2,4,96,768]{3,2,1,0:T(8,128)(2,1)S(1)}, bf16[2,4,96,768]{3,2,1,0:T(8,128)(2,1)S(1)}, u32[]{:S(2)}, u32[]{:S(2)}) collective-permute-start(bf16[2,4,96,768]{3,2,1,0:T(8,128)(2,1)S(1)} %fusion.59), channel_id=1, source_target_pairs={{0,1},{1,2},{2,3},{4,5},{5,6},{6,7}} | collective-permute-start | bytes 3538952 | tf_op jit(solution)/shard_map/ppermute | solution.py:26
  33.5 0.7 copy-start.6
  74.7 3.0 %copy-start.5 = (f32[4,768]{1,0:T(4,128)S(1)}, f32[4,768]{1,0:T(4,128)}, u32[]{:S(2)}) copy-start(f32[4,768]{1,0:T(4,128)} %param.13) | copy-start | bytes 36868
  75.5 17.5 %collective-permute-start.1 = (bf16[2,4,96,768]{3,2,1,0:T(8,128)(2,1)S(1)}, bf16[2,4,96,768]{3,2,1,0:T(8,128)(2,1)S(1)}, u32[]{:S(2)}, u32[]{:S(2)}) collective-permute-start(bf16[2,4,96,768]{3,2,1,0:T(8,128)(2,1)S(1)} %multiply_convert_fusion.1), channel_id=1, source_target_pairs={{0,1},{1,2},{2,3},{4,5},{5,6},{6,7}} | collective-permute-start | bytes 3538952 | tf_op jit(solution)/shard_map/ppermute | solution.py:26
  129.1 1.3 copy-start
  143.3 1.8 copy-start.8
  143.3 2.6 copy-start.4
  159.3 17.5 %collective-permute-start.2 = (bf16[2,4,96,768]{3,2,1,0:T(8,128)(2,1)S(1)}, bf16[2,4,96,768]{3,2,1,0:T(8,128)(2,1)S(1)}, u32[]{:S(2)}, u32[]{:S(2)}) collective-permute-start(bf16[2,4,96,768]{3,2,1,0:T(8,128)(2,1)S(1)} %fusion.72), channel_id=1, source_target_pairs={{0,1},{1,2},{2,3},{4,5},{5,6},{6,7}} | collective-permute-start | bytes 3538952 | tf_op jit(solution)/shard_map/ppermute | solution.py:26
  179.9 0.7 copy-start.7
  222.7 0.7 copy-start.1
  224.2 17.5 %collective-permute-start.3 = (bf16[2,4,96,768]{3,2,1,0:T(8,128)(2,1)S(1)}, bf16[2,4,96,768]{3,2,1,0:T(8,128)(2,1)S(1)}, u32[]{:S(2)}, u32[]{:S(2)}) collective-permute-start(bf16[2,4,96,768]{3,2,1,0:T(8,128)(2,1)S(1)} %multiply_convert_fusion), channel_id=1, source_target_pairs={{0,1},{1,2},{2,3},{4,5},{5,6},{6,7}} | collective-permute-start | bytes 3538952 | tf_op jit(solution)/shard_map/ppermute | solution.py:26
  280.7 0.7 copy-start.2
where the time goes:
time: 288 us; the launch traced here: 283 us
  matrix products  139 us (48%)
  waiting for transfers between devices  60.8 us (21%)
  local copies, waits for them, and re-layouts  31.6 us (11%)
  blocking collectives  29.3 us (10%)
  other arithmetic  13.8 us (5%)
  starting transfers between devices  7.85 us (3%)
    conv_general_dilated x4, matrix products, halo_conv(): lax.conv_general_dilated(padded[None], kernel, (1, 1, 1), ((0, 0), (1, 1)...  129 us
    ppermute x4, waiting for transfers between devices, halo_conv(): lax.ppermute(activation[-2:], 'time', [(source, source + 1) for source in...  60.8 us
    psum x5, blocking collectives, norm_full(): totals = lax.psum(group_stats(feature), 'time')  29.3 us
    conv_general_dilated x16, local copies, waits for them, and re-layouts, halo_conv(): lax.conv_general_dilated(padded[None], kernel, (1, 1, 1), ((0, 0), (1, 1)...  10.7 us
    unnamed x22, local copies, waits for them, and re-layouts  10.1 us
    ppermute x4, starting transfers between devices, halo_conv(): lax.ppermute(activation[-2:], 'time', [(source, source + 1) for source in...  7.85 us
  transfers between devices with their start and end apart: 4, of which 4 were waited for; matrix products, arithmetic and copies ran while one was open for 0% of the time, Pallas kernels for 0%

commit v1 on v0

v1 whole, which is shorter than its diff:
```python
import jax
import jax.numpy as jnp
from jax import lax
from jax.experimental import pallas as pl
from jax.experimental.pallas import tpu as pltpu
from jax.sharding import PartitionSpec as P

GROUPS = 32
NORM_EPS = 1e-6
MESH = pl.DeviceIdType.MESH
BF = jnp.bfloat16
F32 = jnp.float32
RING = 4


def make_kernel(group_size, height, width, channels):
    C = channels
    NT = C // 256
    FR = height * width
    assert height == 4
    elem_count = float(group_size * 2 * FR * (C // GROUPS))
    units_conv = 3 * NT
    units_all = 4 * units_conv

    def body(latent, conv_w, conv_b, norm_g, norm_b, attn_w, attn_b, gmask, out,
             wbuf, awbuf, xs, xres, hbuf, halo, acc, qkv, stat, norm,
             wsem, awsem, insem, outsem, hsend, hrecv, ssend, srecv):
        me = lax.axis_index("time")

        def weight_copies(u):
            conv = u // units_conv
            rest = lax.rem(u, units_conv)
            tap_t = 2 - rest // NT
            tile = lax.rem(rest, NT)
            slot = lax.rem(u, RING)
            return [pltpu.make_async_copy(
                conv_w.at[conv, tap_t, d, :, :, pl.ds(pl.multiple_of(tile * 256, 256), 256)],
                wbuf.at[slot, d], wsem.at[slot, d]) for d in range(3)]

        def attn_weight_copy():
            return pltpu.make_async_copy(attn_w, awbuf, awsem)

        def in_copy(n):
            return pltpu.make_async_copy(latent.at[:, pl.ds(n * 256, 256)], xres.at[n], insem.at[n])

        def out_copy(n):
            return pltpu.make_async_copy(xres.at[n], out.at[:, pl.ds(n * 256, 256)], outsem.at[n])

        def halo_copy(src, conv, n, f):
            return pltpu.make_async_remote_copy(
                src_ref=src.at[n, pl.ds(f * FR, FR)],
                dst_ref=halo.at[conv, n, pl.ds(f * FR, FR)],
                send_sem=hsend.at[conv, n, f], recv_sem=hrecv.at[conv, n, f],
                device_id={"time": lax.rem(me + 1, group_size)}, device_id_type=MESH)

        def halo_start(src, conv, n):
            @pl.when(me < group_size - 1)
            def _():
                for f in (1, 0):
                    halo_copy(src, conv, n, f).start()

        def halo_wait_send(src, conv):
            @pl.when(me < group_size - 1)
            def _():
                for n in range(NT):
                    for f in (1, 0):
                        halo_copy(src, conv, n, f).wait_send()

        def stat_copy(g, p):
            return pltpu.make_async_remote_copy(
                src_ref=stat.at[g, me], dst_ref=stat.at[g, me],
                send_sem=ssend.at[g, p], recv_sem=srecv.at[g, p],
                device_id={"time": lax.rem(me + p, group_size)}, device_id_type=MESH)

        for n in range(NT):
            in_copy(n).start()
        for u in range(RING):
            for c in weight_copies(u):
                c.start()
        attn_weight_copy().start()

        barrier = pltpu.get_barrier_semaphore()
        for p in range(1, group_size):
            pl.semaphore_signal(barrier, inc=1, device_id={"time": lax.rem(me + p, group_size)}, device_id_type=MESH)

        def tile_cols(n):
            return pl.ds(n * 256 if isinstance(n, int) else pl.multiple_of(n * 256, 256), 256)

        def put_stats(g, n, s1, s2):
            stat[g, me, 0:1, tile_cols(n)] = jnp.sum(s1, axis=0, keepdims=True)
            stat[g, me, 1:2, tile_cols(n)] = jnp.sum(s2, axis=0, keepdims=True)

        def fold(v):
            return jnp.sum(v.reshape(v.shape[0] // 8, 8, v.shape[1]), axis=0)

        def exchange(g):
            for p in range(1, group_size):
                stat_copy(g, p).start()
            for p in range(1, group_size):
                stat_copy(g, p).wait_recv()
            total = stat[g, 0]
            for r in range(1, group_size):
                total = total + stat[g, r]
            for p in range(1, group_size):
                stat_copy(g, p).wait_send()

            def left(v, k):
                return pltpu.roll(v, C - k, 1)

            s = total + left(total, 1)
            s = s + left(s, 2)
            s = s + left(s, 4)
            s = s + left(s, 8) + left(s, 16)
            s = jnp.where(gmask[...] > 0.5, s, 0.0)
            s = s + pltpu.roll(s, 1, 1)
            s = s + pltpu.roll(s, 2, 1)
            s = s + pltpu.roll(s, 4, 1)
            s = s + pltpu.roll(s, 8, 1) + pltpu.roll(s, 16, 1)
            mean = s[0:1] / elem_count
            var = s[1:2] / elem_count - mean * mean
            norm[0:1] = mean
            norm[1:2] = lax.rsqrt(var + NORM_EPS) * norm_g[pl.ds(g, 1)]
            norm[2:3] = norm_b[pl.ds(g, 1)]

        def normed(v, k):
            cols = pl.ds(k * 256, 256)
            return (v.astype(F32) - norm[0:1, cols]) * norm[1:2, cols] + norm[2:3, cols]

        row_id = lax.broadcasted_iota(jnp.int32, (width, 256), 0)

        def activate(src, frame_slot, f, row):
            at = pl.ds(pl.multiple_of((frame_slot * height + row) * width, width), width)
            for k in range(NT):
                z = normed(src[k, pl.ds(pl.multiple_of((f * height + row) * width, width), width), :], k)
                z = z * lax.logistic(z)
                xs[at, C + k * 256:C + (k + 1) * 256] = z.astype(BF)
                xs[at, k * 256:(k + 1) * 256] = jnp.where(row_id == 0, 0.0, pltpu.roll(z, 1, 0)).astype(BF)
                xs[at, 2 * C + k * 256:2 * C + (k + 1) * 256] = jnp.where(row_id == width - 1, 0.0, pltpu.roll(z, width - 1, 0)).astype(BF)

        def trip(slot, tap_t, n):
            for d in (1, 0, 2):
                w = wbuf[slot, d].reshape(3 * C, 256)
                if d == 1:
                    lhs = xs[pl.ds(pl.multiple_of(tap_t * FR, FR), 2 * FR), :]
                    acc[n] += jnp.dot(lhs, w, preferred_element_type=F32)
                else:
                    tall = FR - width
                    lo, dst = (0, width) if d == 0 else (width, 0)
                    lhs = jnp.concatenate([xs[pl.ds(pl.multiple_of((tap_t + f) * FR, FR) + lo, tall), :] for f in range(2)], axis=0)
                    r = jnp.dot(lhs, w, preferred_element_type=F32)
                    for f in range(2):
                        acc[n, f * FR + dst:f * FR + dst + tall, :] += r[f * tall:(f + 1) * tall]

        def epilogue(conv, n, g):
            bias = conv_b[pl.ds(conv, 1), tile_cols(n)]

            def rows_out(j, carry):
                rows = pl.ds(pl.multiple_of(j * width, width), width)
                h = (acc[n, rows, :] + bias).astype(BF)
                acc[n, rows, :] = jnp.zeros((width, 256), F32)
                if conv % 2 == 0:
                    hbuf[n, rows, :] = h
                else:
                    h = (xres[n, rows, :].astype(F32) + h.astype(F32)).astype(BF)
                    xres[n, rows, :] = h
                if g is None:
                    return carry
                hf = h.astype(F32)
                return carry[0] + fold(hf), carry[1] + fold(hf * hf)

            s1, s2 = lax.fori_loop(0, 2 * height, rows_out, (jnp.zeros((8, 256), F32), jnp.zeros((8, 256), F32)))
            if g is not None:
                put_stats(g, n, s1, s2)

        def conv(c, src, g_out):
            base = c * units_conv

            def own_rows(j, carry):
                activate(src, 2 + j // height, j // height, lax.rem(j, height))
                return carry

            lax.fori_loop(0, 2 * height, own_rows, 0)

            def get_halo(f):
                @pl.when(me == 0)
                def _():
                    def copy_row(j, carry):
                        xs[pl.ds(pl.multiple_of((f * height + j) * width, width), width), :] = (
                            xs[pl.ds(pl.multiple_of((2 * height + j) * width, width), width), :])
                        return carry
                    lax.fori_loop(0, height, copy_row, 0)

                @pl.when(me > 0)
                def _():
                    for n in range(NT):
                        halo_copy(src, c, n, f).wait_recv()

                    def halo_rows(j, carry):
                        activate(halo.at[c], f, f, j)
                        return carry

                    lax.fori_loop(0, height, halo_rows, 0)

            def step(t, carry):
                @pl.when(t == NT)
                def _():
                    get_halo(1)

                @pl.when(t == 2 * NT)
                def _():
                    get_halo(0)
                    halo_wait_send(src, c)

                u = base + t
                n = lax.rem(t, NT)
                for w in weight_copies(u):
                    w.wait()
                trip(lax.rem(u, RING), 2 - t // NT, n)

                @pl.when(u + RING < units_all)
                def _():
                    for w in weight_copies(u + RING):
                        w.start()

                @pl.when(t >= 2 * NT)
                def _():
                    epilogue(c, n, g_out)
                    if c % 2 == 0:
                        halo_start(hbuf, c + 1, n)
                return carry

            lax.fori_loop(0, 3 * NT, step, 0)

        def attention(g):
            def rows_norm(j, carry):
                at = pl.ds(pl.multiple_of(j * width, width), width)
                for k in range(NT):
                    xs[at, k * 256:(k + 1) * 256] = normed(xres[k, at, :], k).astype(BF)
                return carry

            lax.fori_loop(0, 2 * height, rows_norm, 0)
            attn_weight_copy().wait()
            for w in range(3):
                for n in range(NT):
                    cols = slice(n * 256, (n + 1) * 256)
                    v = jnp.dot(xs[0:2 * FR, 0:C], awbuf[w, :, cols], preferred_element_type=F32) + attn_b[w:w + 1, cols]
                    qkv[w, :, cols] = v.astype(BF)
            for f in range(2):
                rows = slice(f * FR, (f + 1) * FR)
                scores = lax.dot_general(qkv[0, rows, :], qkv[1, rows, :], (((1,), (1,)), ((), ())), preferred_element_type=F32)
                scores = scores * (C ** -0.5)
                e = jnp.exp(scores - jnp.max(scores, axis=1, keepdims=True))
                probs = (e / jnp.sum(e, axis=1, keepdims=True)).astype(BF)
                xs[rows, C:2 * C] = jnp.dot(probs, qkv[2, rows, :], preferred_element_type=F32).astype(BF)
            for n in range(NT):
                cols = slice(n * 256, (n + 1) * 256)
                h = (jnp.dot(xs[0:2 * FR, C:2 * C], awbuf[3, :, cols], preferred_element_type=F32) + attn_b[3:4, cols]).astype(BF)
                h = (xres[n].astype(F32) + h.astype(F32)).astype(BF)
                xres[n] = h
                hf = h.astype(F32)
                put_stats(g + 1, n, fold(hf), fold(hf * hf))
                halo_start(xres, 2, n)

        for n in range(NT):
            acc[n] = jnp.zeros((2 * FR, 256), F32)
        for g in range(5):
            stat[g, me] = jnp.zeros((8, C), F32)
        for n in range(NT):
            in_copy(n).wait()
        pl.semaphore_wait(barrier, group_size - 1)
        for n in range(NT):
            halo_start(xres, 0, n)
        for n in range(NT):
            def in_stats(j, carry):
                v = xres[n, pl.ds(pl.multiple_of(j * width, width), width), :].astype(F32)
                return carry[0] + fold(v), carry[1] + fold(v * v)

            s1, s2 = lax.fori_loop(0, 2 * height, in_stats, (jnp.zeros((8, 256), F32), jnp.zeros((8, 256), F32)))
            put_stats(0, n, s1, s2)
        exchange(0)
        conv(0, xres, 1)
        exchange(1)
        conv(1, hbuf, 2)
        exchange(2)
        attention(2)
        exchange(3)
        conv(2, xres, 4)
        exchange(4)
        conv(3, hbuf, None)
        for n in range(NT):
            out_copy(n).start()
        for n in range(NT):
            out_copy(n).wait()

    scratch = [
        pltpu.VMEM((RING, 3, 3, C, 256), BF),
        pltpu.VMEM((4, C, C), BF),
        pltpu.VMEM((4 * FR, 3 * C), BF),
        pltpu.VMEM((NT, 2 * FR, 256), BF),
        pltpu.VMEM((NT, 2 * FR, 256), BF),
        pltpu.VMEM((4, NT, 2 * FR, 256), BF),
        pltpu.VMEM((NT, 2 * FR, 256), F32),
        pltpu.VMEM((3, 2 * FR, C), BF),
        pltpu.VMEM((5, group_size, 8, C), F32),
        pltpu.VMEM((8, C), F32),
        pltpu.SemaphoreType.DMA((RING, 3)),
        pltpu.SemaphoreType.DMA,
        pltpu.SemaphoreType.DMA((NT,)),
        pltpu.SemaphoreType.DMA((NT,)),
        pltpu.SemaphoreType.DMA((4, NT, 2)),
        pltpu.SemaphoreType.DMA((4, NT, 2)),
        pltpu.SemaphoreType.DMA((5, group_size)),
        pltpu.SemaphoreType.DMA((5, group_size)),
    ]
    return body, scratch


def solution(mesh):
    group_size = mesh.shape["time"]
    video_spec = P(("batch", "time"), None, None, None)

    def device_body(latent, conv_w, conv_b, norm_g, norm_b, attn_w, attn_b):
        frames, height, width, channels = latent.shape
        body, scratch = make_kernel(group_size, height, width, channels)
        gmask = jnp.broadcast_to((jnp.arange(channels) % (channels // GROUPS) == 0).astype(F32), (8, channels))
        hbm = pl.BlockSpec(memory_space=pltpu.HBM)
        vmem = pl.BlockSpec(memory_space=pltpu.VMEM)
        out = pl.pallas_call(
            body,
            out_shape=jax.ShapeDtypeStruct((frames * height * width, channels), BF),
            in_specs=[hbm, hbm, vmem, vmem, vmem, hbm, vmem, vmem],
            out_specs=hbm,
            scratch_shapes=scratch,
            compiler_params=pltpu.CompilerParams(collective_id=0, has_side_effects=True, vmem_limit_bytes=60 * 1024 * 1024),
            name="mid_block",
        )(latent.reshape(frames * height * width, channels), conv_w, conv_b, norm_g, norm_b, attn_w, attn_b, gmask)
        return out.reshape(latent.shape)

    return jax.shard_map(device_body, mesh=mesh, in_specs=(video_spec, P(), P(), P(), P(), P(), P()), out_specs=video_spec, check_vma=False)
```

time: 288 us -> 170 us (0.59)
  the two profiles are of different devices: /device:TPU:6 before, /device:TPU:7 now
where the time goes in v1:
time: 170 us
  Pallas kernels  167 us (98%)
  local copies, waits for them, and re-layouts  2.97 us (2%)
    pallas_call x1, Pallas kernels, device_body(): pl.pallas_call(body, out_shape=jax.ShapeDtypeStruct((frames * height * wi...  167 us

profile of v1, /device:TPU:7, one launch (start us, length us, event | category | flops | bytes accessed | tf_op | source)
XLA Modules:
  0.0 169.9 jit_solution(11320683520695479115)
XLA Ops:
  0.0 0.6 broadcast_in_dim.3.gmask
  0.6 166.9 %mid_block.1 = bf16[768,768]{1,0:T(8,128)(2,1)} custom-call(bf16[768,768]{1,0:T(8,128)(2,1)} %bitcast.3, bf16[4,3,3,3,768,768]{5,4,3,2,1,0:T(8,128)(2,1)} %conv_w.1, f32[4,768]{1,0:T(4,128)} %conv_b.1, f32[5,768]{1,0:T(8,128)} %norm_g.1, f32[5,768]{1,0:T(8,128)} %norm_b.1, bf16[4,768,768]{2,1,0:T(8,128)(2,1)} %attn_w.1, f32[4,768]{1,0:T(4,128)} %attn_b.1, ...), custom_call_target="tpu_custom_call" | custom-call | tf_op jit(solution)/shard_map/mid_block/pallas_call | solution.py:328
  167.5 2.4 %copy.9 = bf16[2,4,96,768]{3,2,1,0:T(8,128)(2,1)} copy(bf16[2,4,96,768]{3,2,1,0:T(8,128)(2,1)} %bitcast.2) | data formatting | bytes 2359296
  (1 shorter events, 0.0 us)

commit v2 on v1

--- a/solution.py
+++ b/solution.py
@@ -22,7 +22,7 @@
     units_conv = 3 * NT
     units_all = 4 * units_conv
 
-    def body(latent, conv_w, conv_b, norm_g, norm_b, attn_w, attn_b, gmask, out,
+    def body(latent, conv_w, conv_b, norm_g, norm_b, attn_w, attn_b, out,
              wbuf, awbuf, xs, xres, hbuf, halo, acc, qkv, stat, norm,
              wsem, awsem, insem, outsem, hsend, hrecv, ssend, srecv):
         me = lax.axis_index("time")
@@ -53,11 +53,12 @@
                 send_sem=hsend.at[conv, n, f], recv_sem=hrecv.at[conv, n, f],
                 device_id={"time": lax.rem(me + 1, group_size)}, device_id_type=MESH)
 
-        def halo_start(src, conv, n):
+        def halo_start(src, conv):
             @pl.when(me < group_size - 1)
             def _():
                 for f in (1, 0):
-                    halo_copy(src, conv, n, f).start()
+                    for n in range(NT):
+                        halo_copy(src, conv, n, f).start()
 
         def halo_wait_send(src, conv):
             @pl.when(me < group_size - 1)
@@ -93,9 +94,26 @@
         def fold(v):
             return jnp.sum(v.reshape(v.shape[0] // 8, 8, v.shape[1]), axis=0)
 
-        def exchange(g):
+        lane = lax.broadcasted_iota(jnp.int32, (8, 128), 1)
+
+        def group_totals(v):
+            size = C // GROUPS
+            parts = [v[:, i * 128:(i + 1) * 128] for i in range(C // 128)]
+            done = [jnp.zeros((8, 128), F32) for _ in parts]
+            for q in range(GROUPS):
+                lo, hi = q * size, (q + 1) * size
+                inside = [(i, (lane >= lo - i * 128) & (lane < hi - i * 128)) for i in range(lo // 128, (hi - 1) // 128 + 1)]
+                picked = sum(jnp.where(m, parts[i], 0.0) for i, m in inside)
+                total = jnp.sum(picked, axis=1, keepdims=True)
+                for i, m in inside:
+                    done[i] = jnp.where(m, total, done[i])
+            return jnp.concatenate(done, axis=1)
+
+        def exchange(g, then=None):
             for p in range(1, group_size):
                 stat_copy(g, p).start()
+            if then is not None:
+                then()
             for p in range(1, group_size):
                 stat_copy(g, p).wait_recv()
             total = stat[g, 0]
@@ -103,19 +121,7 @@
                 total = total + stat[g, r]
             for p in range(1, group_size):
                 stat_copy(g, p).wait_send()
-
-            def left(v, k):
-                return pltpu.roll(v, C - k, 1)
-
-            s = total + left(total, 1)
-            s = s + left(s, 2)
-            s = s + left(s, 4)
-            s = s + left(s, 8) + left(s, 16)
-            s = jnp.where(gmask[...] > 0.5, s, 0.0)
-            s = s + pltpu.roll(s, 1, 1)
-            s = s + pltpu.roll(s, 2, 1)
-            s = s + pltpu.roll(s, 4, 1)
-            s = s + pltpu.roll(s, 8, 1) + pltpu.roll(s, 16, 1)
+            s = group_totals(total)
             mean = s[0:1] / elem_count
             var = s[1:2] / elem_count - mean * mean
             norm[0:1] = mean
@@ -225,8 +231,6 @@
                 @pl.when(t >= 2 * NT)
                 def _():
                     epilogue(c, n, g_out)
-                    if c % 2 == 0:
-                        halo_start(hbuf, c + 1, n)
                 return carry
 
             lax.fori_loop(0, 3 * NT, step, 0)
@@ -259,7 +263,6 @@
                 xres[n] = h
                 hf = h.astype(F32)
                 put_stats(g + 1, n, fold(hf), fold(hf * hf))
-                halo_start(xres, 2, n)
 
         for n in range(NT):
             acc[n] = jnp.zeros((2 * FR, 256), F32)
@@ -269,23 +272,21 @@
             in_copy(n).wait()
         pl.semaphore_wait(barrier, group_size - 1)
         for n in range(NT):
-            halo_start(xres, 0, n)
-        for n in range(NT):
             def in_stats(j, carry):
                 v = xres[n, pl.ds(pl.multiple_of(j * width, width), width), :].astype(F32)
                 return carry[0] + fold(v), carry[1] + fold(v * v)
 
             s1, s2 = lax.fori_loop(0, 2 * height, in_stats, (jnp.zeros((8, 256), F32), jnp.zeros((8, 256), F32)))
             put_stats(0, n, s1, s2)
-        exchange(0)
+        exchange(0, lambda: halo_start(xres, 0))
         conv(0, xres, 1)
-        exchange(1)
+        exchange(1, lambda: halo_start(hbuf, 1))
         conv(1, hbuf, 2)
         exchange(2)
         attention(2)
-        exchange(3)
+        exchange(3, lambda: halo_start(xres, 2))
         conv(2, xres, 4)
-        exchange(4)
+        exchange(4, lambda: halo_start(hbuf, 3))
         conv(3, hbuf, None)
         for n in range(NT):
             out_copy(n).start()
@@ -322,18 +323,17 @@
     def device_body(latent, conv_w, conv_b, norm_g, norm_b, attn_w, attn_b):
         frames, height, width, channels = latent.shape
         body, scratch = make_kernel(group_size, height, width, channels)
-        gmask = jnp.broadcast_to((jnp.arange(channels) % (channels // GROUPS) == 0).astype(F32), (8, channels))
         hbm = pl.BlockSpec(memory_space=pltpu.HBM)
         vmem = pl.BlockSpec(memory_space=pltpu.VMEM)
         out = pl.pallas_call(
             body,
             out_shape=jax.ShapeDtypeStruct((frames * height * width, channels), BF),
-            in_specs=[hbm, hbm, vmem, vmem, vmem, hbm, vmem, vmem],
+            in_specs=[hbm, hbm, vmem, vmem, vmem, hbm, vmem],
             out_specs=hbm,
             scratch_shapes=scratch,
             compiler_params=pltpu.CompilerParams(collective_id=0, has_side_effects=True, vmem_limit_bytes=60 * 1024 * 1024),
             name="mid_block",
-        )(latent.reshape(frames * height * width, channels), conv_w, conv_b, norm_g, norm_b, attn_w, attn_b, gmask)
+        )(latent.reshape(frames * height * width, channels), conv_w, conv_b, norm_g, norm_b, attn_w, attn_b)
         return out.reshape(latent.shape)
 
     return jax.shard_map(device_body, mesh=mesh, in_specs=(video_spec, P(), P(), P(), P(), P(), P()), out_specs=video_spec, check_vma=False)

time: 170 us -> 135 us (0.79)
  the two profiles are of different devices: /device:TPU:7 before, /device:TPU:0 now
where the time goes in v2:
time: 135 us
  Pallas kernels  132 us (98%)
  local copies, waits for them, and re-layouts  2.36 us (2%)
    pallas_call x1, Pallas kernels, device_body(): pl.pallas_call(body, out_shape=jax.ShapeDtypeStruct((frames * height * wi...  132 us

profile of v2, /device:TPU:0, one launch (start us, length us, event | category | flops | bytes accessed | tf_op | source)
XLA Modules:
  0.0 134.7 jit_solution(13335482633200278684)
XLA Ops:
  0.0 132.3 %mid_block.1 = bf16[768,768]{1,0:T(8,128)(2,1)} custom-call(bf16[768,768]{1,0:T(8,128)(2,1)} %bitcast.3, bf16[4,3,3,3,768,768]{5,4,3,2,1,0:T(8,128)(2,1)} %conv_w.1, f32[4,768]{1,0:T(4,128)} %conv_b.1, f32[5,768]{1,0:T(8,128)} %norm_g.1, f32[5,768]{1,0:T(8,128)} %norm_b.1, bf16[4,768,768]{2,1,0:T(8,128)(2,1)} %attn_w.1, f32[4,768]{1,0:T(4,128)} %attn_b.1), custom_call_target="tpu_custom_call" | custom-call | tf_op jit(solution)/shard_map/mid_block/pallas_call | solution.py:328
  132.4 2.4 %copy.9 = bf16[2,4,96,768]{3,2,1,0:T(8,128)(2,1)} copy(bf16[2,4,96,768]{3,2,1,0:T(8,128)(2,1)} %bitcast.2) | data formatting | bytes 2359296

commit v3 on v2

v3 whole, which is shorter than its diff:
```python
import jax
import jax.numpy as jnp
from jax import lax
from jax.experimental import pallas as pl
from jax.experimental.pallas import tpu as pltpu
from jax.sharding import PartitionSpec as P

GROUPS = 32
NORM_EPS = 1e-6
MESH = pl.DeviceIdType.MESH
BF = jnp.bfloat16
F32 = jnp.float32
RING = 6


def make_kernel(group_size, height, width, channels):
    C = channels
    NT = C // 256
    FR = height * width
    assert height == 4
    elem_count = float(group_size * 2 * FR * (C // GROUPS))
    units_conv = 3 * NT
    units_all = 4 * units_conv

    def body(latent, conv_w, conv_b, norm_g, norm_b, attn_w, attn_b, out,
             wbuf, awbuf, xs0, xs1, xs2, xs3, buf, halo, acc, qkv, stat, norm,
             wsem, awsem, insem, outsem, hsend, hrecv, ssend, srecv):
        me = lax.axis_index("time")
        xs = (xs0, xs1, xs2, xs3)
        xres = buf.at[0]

        def weight_copies(u):
            conv = u // units_conv
            rest = lax.rem(u, units_conv)
            tap_t = 2 - rest // NT
            tile = lax.rem(rest, NT)
            slot = lax.rem(u, RING)
            return [pltpu.make_async_copy(
                conv_w.at[conv, tap_t, d, :, :, pl.ds(pl.multiple_of(tile * 256, 256), 256)],
                wbuf.at[slot, d], wsem.at[slot, d]) for d in range(3)]

        def attn_weight_copy():
            return pltpu.make_async_copy(attn_w, awbuf, awsem)

        def in_copy(n):
            return pltpu.make_async_copy(latent.at[:, pl.ds(n * 256, 256)], xres.at[n], insem.at[n])

        def out_copy(n):
            return pltpu.make_async_copy(xres.at[n], out.at[:, pl.ds(n * 256, 256)], outsem.at[n])

        def halo_copy(conv, n, f):
            return pltpu.make_async_remote_copy(
                src_ref=buf.at[lax.rem(conv, 2), n, pl.ds(f * FR, FR)],
                dst_ref=halo.at[conv, n, pl.ds(f * FR, FR)],
                send_sem=hsend.at[conv, n, f], recv_sem=hrecv.at[conv, n, f],
                device_id={"time": lax.rem(me + 1, group_size)}, device_id_type=MESH)

        def first_copy(conv, n, f):
            return pltpu.make_async_copy(
                buf.at[lax.rem(conv, 2), n, pl.ds(0, FR)], halo.at[conv, n, pl.ds(f * FR, FR)], hrecv.at[conv, n, f])

        def halo_start(conv):
            @pl.when(me < group_size - 1)
            def _():
                for f in (1, 0):
                    for n in range(NT):
                        halo_copy(conv, n, f).start()

            @pl.when(me == 0)
            def _():
                for f in (1, 0):
                    for n in range(NT):
                        first_copy(conv, n, f).start()

        def halo_wait(conv, f):
            @pl.when(me == 0)
            def _():
                for n in range(NT):
                    first_copy(conv, n, f).wait()

            @pl.when(me > 0)
            def _():
                for n in range(NT):
                    halo_copy(conv, n, f).wait_recv()

        def halo_wait_send(conv):
            @pl.when(me < group_size - 1)
            def _():
                for n in range(NT):
                    for f in (1, 0):
                        halo_copy(conv, n, f).wait_send()

        def stat_copy(g, p):
            return pltpu.make_async_remote_copy(
                src_ref=stat.at[g, me], dst_ref=stat.at[g, me],
                send_sem=ssend.at[g, p], recv_sem=srecv.at[g, p],
                device_id={"time": lax.rem(me + p, group_size)}, device_id_type=MESH)

        for n in range(NT):
            in_copy(n).start()
        for u in range(RING):
            for c in weight_copies(u):
                c.start()
        attn_weight_copy().start()

        barrier = pltpu.get_barrier_semaphore()
        for p in range(1, group_size):
            pl.semaphore_signal(barrier, inc=1, device_id={"time": lax.rem(me + p, group_size)}, device_id_type=MESH)

        def tile_cols(n):
            return pl.ds(n * 256 if isinstance(n, int) else pl.multiple_of(n * 256, 256), 256)

        def put_stats(g, n, s1, s2):
            stat[g, me, 0:1, tile_cols(n)] = jnp.sum(s1, axis=0, keepdims=True)
            stat[g, me, 1:2, tile_cols(n)] = jnp.sum(s2, axis=0, keepdims=True)

        def fold(v):
            return jnp.sum(v.reshape(v.shape[0] // 8, 8, v.shape[1]), axis=0)

        lane = lax.broadcasted_iota(jnp.int32, (8, 128), 1)

        def group_totals(v):
            size = C // GROUPS
            parts = [v[:, i * 128:(i + 1) * 128] for i in range(C // 128)]
            done = [jnp.zeros((8, 128), F32) for _ in parts]
            for q in range(GROUPS):
                lo, hi = q * size, (q + 1) * size
                inside = [(i, (lane >= lo - i * 128) & (lane < hi - i * 128)) for i in range(lo // 128, (hi - 1) // 128 + 1)]
                picked = sum(jnp.where(m, parts[i], 0.0) for i, m in inside)
                total = jnp.sum(picked, axis=1, keepdims=True)
                for i, m in inside:
                    done[i] = jnp.where(m, total, done[i])
            return jnp.concatenate(done, axis=1)

        def exchange(g, then=None):
            for p in range(1, group_size):
                stat_copy(g, p).start()
            if then is not None:
                then()
            for p in range(1, group_size):
                stat_copy(g, p).wait_recv()
            total = stat[g, 0]
            for r in range(1, group_size):
                total = total + stat[g, r]
            for p in range(1, group_size):
                stat_copy(g, p).wait_send()
            s = group_totals(total)
            mean = s[0:1] / elem_count
            var = s[1:2] / elem_count - mean * mean
            norm[0:1] = mean
            norm[1:2] = lax.rsqrt(var + NORM_EPS) * norm_g[pl.ds(g, 1)]
            norm[2:3] = norm_b[pl.ds(g, 1)]

        def normed(v, k):
            cols = pl.ds(k * 256, 256)
            return (v.astype(F32) - norm[0:1, cols]) * norm[1:2, cols] + norm[2:3, cols]

        row_id = lax.broadcasted_iota(jnp.int32, (width, 256), 0)

        def activate(src, slot, f, k):
            for row in range(height):
                rows = slice(row * width, (row + 1) * width)
                z = normed(src[k, f * FR + row * width:f * FR + (row + 1) * width, :], k)
                z = z * lax.logistic(z)
                at = k * 3 * 256
                xs[slot][rows, at:at + 256] = jnp.where(row_id == 0, 0.0, pltpu.roll(z, 1, 0)).astype(BF)
                xs[slot][rows, at + 256:at + 512] = z.astype(BF)
                xs[slot][rows, at + 512:at + 768] = jnp.where(row_id == width - 1, 0.0, pltpu.roll(z, width - 1, 0)).astype(BF)

        def trip(slot, tap_t, n):
            for d in (1, 0, 2):
                w = jnp.concatenate([wbuf[slot, d, e, k * 256:(k + 1) * 256, :] for k in range(NT) for e in range(3)], axis=0)
                rows = FR if d == 1 else FR - width
                lo, dst = {0: (0, width), 1: (0, 0), 2: (width, 0)}[d]
                lhs = jnp.concatenate([xs[tap_t + f][lo:lo + rows, :] for f in range(2)], axis=0)
                r = jnp.dot(lhs, w, preferred_element_type=F32)
                if d == 1 and tap_t == 2:
                    acc[n] = r
                else:
                    for f in range(2):
                        acc[n, f * FR + dst:f * FR + dst + rows, :] += r[f * rows:(f + 1) * rows]

        def epilogue(c, n, g):
            odd = lax.rem(c, 2)
            bias = conv_b[pl.ds(c, 1), n * 256:(n + 1) * 256]
            keep = odd.astype(F32)
            s1 = jnp.zeros((8, 256), F32)
            s2 = jnp.zeros((8, 256), F32)
            for j in range(2 * height):
                rows = slice(j * width, (j + 1) * width)
                h = (acc[n, rows, :] + bias).astype(BF).astype(F32)
                h = (xres[n, rows, :].astype(F32) * keep + h).astype(BF)
                buf[1 - odd, n, rows, :] = h
                hf = h.astype(F32)
                s1 = s1 + fold(hf)
                s2 = s2 + fold(hf * hf)
            put_stats(g, n, s1, s2)

        def conv(c):
            base = c * units_conv
            g_in = c + c // 2
            src = buf.at[lax.rem(c, 2)]

            exchange(g_in, lambda: halo_start(c))

            for tap_t in (2, 1, 0):
                first = base + (2 - tap_t) * NT
                for n in range(NT):
                    for w in weight_copies(first + n):
                        w.wait()
                if tap_t < 2:
                    halo_wait(c, tap_t)
                if tap_t == 0:
                    halo_wait_send(c)

                @pl.when(me < group_size)
                def _():
                    if tap_t == 2:
                        for k in range(NT):
                            for f in range(2):
                                activate(src, 2 + f, f, k)
                    else:
                        for k in range(NT):
                            activate(halo.at[c], tap_t, tap_t, k)
                    for n in range(NT):
                        trip(lax.rem(first + n, RING), tap_t, n)
                        if tap_t == 0:
                            epilogue(c, n, g_in + 1)

                for n in range(NT):
                    @pl.when(first + n + RING < units_all)
                    def _():
                        for w in weight_copies(first + n + RING):
                            w.start()

        def attention(g):
            def rows_norm(j, carry):
                at = pl.ds(pl.multiple_of(j * width, width), width)
                for k in range(NT):
                    qkv[3, at, k * 256:(k + 1) * 256] = normed(xres[k, at, :], k).astype(BF)
                return carry

            lax.fori_loop(0, 2 * height, rows_norm, 0)
            attn_weight_copy().wait()
            for w in range(3):
                for n in range(NT):
                    cols = slice(n * 256, (n + 1) * 256)
                    v = jnp.dot(qkv[3], awbuf[w, :, cols], preferred_element_type=F32) + attn_b[w:w + 1, cols]
                    qkv[w, :, cols] = v.astype(BF)
            for f in range(2):
                rows = slice(f * FR, (f + 1) * FR)
                scores = lax.dot_general(qkv[0, rows, :], qkv[1, rows, :], (((1,), (1,)), ((), ())), preferred_element_type=F32)
                scores = scores * (C ** -0.5)
                e = jnp.exp(scores - jnp.max(scores, axis=1, keepdims=True))
                probs = (e / jnp.sum(e, axis=1, keepdims=True)).astype(BF)
                qkv[3, rows, :] = jnp.dot(probs, qkv[2, rows, :], preferred_element_type=F32).astype(BF)
            for n in range(NT):
                cols = slice(n * 256, (n + 1) * 256)
                h = (jnp.dot(qkv[3], awbuf[3, :, cols], preferred_element_type=F32) + attn_b[3:4, cols]).astype(BF)
                h = (xres[n].astype(F32) + h.astype(F32)).astype(BF)
                xres[n] = h
                hf = h.astype(F32)
                put_stats(g + 1, n, fold(hf), fold(hf * hf))

        for g in range(6):
            stat[g, me] = jnp.zeros((8, C), F32)
        for n in range(NT):
            in_copy(n).wait()
        pl.semaphore_wait(barrier, group_size - 1)
        for n in range(NT):
            def in_stats(j, carry):
                v = xres[n, pl.ds(pl.multiple_of(j * width, width), width), :].astype(F32)
                return carry[0] + fold(v), carry[1] + fold(v * v)

            s1, s2 = lax.fori_loop(0, 2 * height, in_stats, (jnp.zeros((8, 256), F32), jnp.zeros((8, 256), F32)))
            put_stats(0, n, s1, s2)
        def layer(c, carry):
            conv(c)

            @pl.when(c == 1)
            def _():
                exchange(2)
                attention(2)
            return carry

        lax.fori_loop(0, 4, layer, 0)
        for n in range(NT):
            out_copy(n).start()
        for n in range(NT):
            out_copy(n).wait()

    scratch = [
        pltpu.VMEM((RING, 3, 3, C, 256), BF),
        pltpu.VMEM((4, C, C), BF),
        pltpu.VMEM((FR, 3 * C), BF),
        pltpu.VMEM((FR, 3 * C), BF),
        pltpu.VMEM((FR, 3 * C), BF),
        pltpu.VMEM((FR, 3 * C), BF),
        pltpu.VMEM((2, NT, 2 * FR, 256), BF),
        pltpu.VMEM((4, NT, 2 * FR, 256), BF),
        pltpu.VMEM((NT, 2 * FR, 256), F32),
        pltpu.VMEM((4, 2 * FR, C), BF),
        pltpu.VMEM((6, group_size, 8, C), F32),
        pltpu.VMEM((8, C), F32),
        pltpu.SemaphoreType.DMA((RING, 3)),
        pltpu.SemaphoreType.DMA,
        pltpu.SemaphoreType.DMA((NT,)),
        pltpu.SemaphoreType.DMA((NT,)),
        pltpu.SemaphoreType.DMA((4, NT, 2)),
        pltpu.SemaphoreType.DMA((4, NT, 2)),
        pltpu.SemaphoreType.DMA((5, group_size)),
        pltpu.SemaphoreType.DMA((5, group_size)),
    ]
    return body, scratch


def solution(mesh):
    group_size = mesh.shape["time"]
    video_spec = P(("batch", "time"), None, None, None)

    def device_body(latent, conv_w, conv_b, norm_g, norm_b, attn_w, attn_b):
        frames, height, width, channels = latent.shape
        body, scratch = make_kernel(group_size, height, width, channels)
        hbm = pl.BlockSpec(memory_space=pltpu.HBM)
        vmem = pl.BlockSpec(memory_space=pltpu.VMEM)
        out = pl.pallas_call(
            body,
            out_shape=jax.ShapeDtypeStruct((frames * height * width, channels), BF),
            in_specs=[hbm, hbm, vmem, vmem, vmem, hbm, vmem],
            out_specs=hbm,
            scratch_shapes=scratch,
            compiler_params=pltpu.CompilerParams(collective_id=0, has_side_effects=True, vmem_limit_bytes=60 * 1024 * 1024),
            name="mid_block",
        )(latent.reshape(frames * height * width, channels), conv_w, conv_b, norm_g, norm_b, attn_w, attn_b)
        return out.reshape(latent.shape)

    return jax.shard_map(device_body, mesh=mesh, in_specs=(video_spec, P(), P(), P(), P(), P(), P()), out_specs=video_spec, check_vma=False)
```

time: 135 us -> 125 us (0.926)
  Pallas kernels: 132 us -> 122 us
    pallas_call x1, Pallas kernels: 132 us -> 122 us  [device_body(): pl.pallas_call(body, out_shape=jax.ShapeDtypeStruct((frames * height * wi...]
where the time goes in v3:
time: 125 us
  Pallas kernels  122 us (98%)
  local copies, waits for them, and re-layouts  2.36 us (2%)
    pallas_call x1, Pallas kernels, device_body(): pl.pallas_call(body, out_shape=jax.ShapeDtypeStruct((frames * height * wi...  122 us

profile of v3, /device:TPU:0, one launch (start us, length us, event | category | flops | bytes accessed | tf_op | source)
XLA Modules:
  0.0 124.8 jit_solution(213024707894855894)
XLA Ops:
  0.0 122.4 %mid_block.1 = bf16[768,768]{1,0:T(8,128)(2,1)} custom-call(bf16[768,768]{1,0:T(8,128)(2,1)} %bitcast.3, bf16[4,3,3,3,768,768]{5,4,3,2,1,0:T(8,128)(2,1)} %conv_w.1, f32[4,768]{1,0:T(4,128)} %conv_b.1, f32[5,768]{1,0:T(8,128)} %norm_g.1, f32[5,768]{1,0:T(8,128)} %norm_b.1, bf16[4,768,768]{2,1,0:T(8,128)(2,1)} %attn_w.1, f32[4,768]{1,0:T(4,128)} %attn_b.1), custom_call_target="tpu_custom_call" | custom-call | tf_op jit(solution)/shard_map/mid_block/pallas_call | solution.py:326
  122.4 2.4 %copy.9 = bf16[2,4,96,768]{3,2,1,0:T(8,128)(2,1)} copy(bf16[2,4,96,768]{3,2,1,0:T(8,128)(2,1)} %bitcast.2) | data formatting | bytes 2359296

commit v4 on v3

--- a/solution.py
+++ b/solution.py
@@ -96,12 +96,13 @@
                 send_sem=ssend.at[g, p], recv_sem=srecv.at[g, p],
                 device_id={"time": lax.rem(me + p, group_size)}, device_id_type=MESH)
 
+        def weights_start(lo, hi):
+            for u in range(lo, hi):
+                for w in weight_copies(u):
+                    w.start()
+
         for n in range(NT):
             in_copy(n).start()
-        for u in range(RING):
-            for c in weight_copies(u):
-                c.start()
-        attn_weight_copy().start()
 
         barrier = pltpu.get_barrier_semaphore()
         for p in range(1, group_size):
@@ -117,12 +118,12 @@
         def fold(v):
             return jnp.sum(v.reshape(v.shape[0] // 8, 8, v.shape[1]), axis=0)
 
-        lane = lax.broadcasted_iota(jnp.int32, (8, 128), 1)
+        lane = lax.broadcasted_iota(jnp.int32, (2, 128), 1)
 
         def group_totals(v):
             size = C // GROUPS
             parts = [v[:, i * 128:(i + 1) * 128] for i in range(C // 128)]
-            done = [jnp.zeros((8, 128), F32) for _ in parts]
+            done = [jnp.zeros((2, 128), F32) for _ in parts]
             for q in range(GROUPS):
                 lo, hi = q * size, (q + 1) * size
                 inside = [(i, (lane >= lo - i * 128) & (lane < hi - i * 128)) for i in range(lo // 128, (hi - 1) // 128 + 1)]
@@ -203,6 +204,10 @@
 
             exchange(g_in, lambda: halo_start(c))
 
+            @pl.when(c == 0)
+            def _():
+                weights_start(NT, RING)
+
             for tap_t in (2, 1, 0):
                 first = base + (2 - tap_t) * NT
                 for n in range(NT):
@@ -227,6 +232,10 @@
                         if tap_t == 0:
                             epilogue(c, n, g_in + 1)
 
+                if tap_t == 1:
+                    @pl.when(c == 0)
+                    def _():
+                        attn_weight_copy().start()
                 for n in range(NT):
                     @pl.when(first + n + RING < units_all)
                     def _():
@@ -262,10 +271,9 @@
                 hf = h.astype(F32)
                 put_stats(g + 1, n, fold(hf), fold(hf * hf))
 
-        for g in range(6):
-            stat[g, me] = jnp.zeros((8, C), F32)
         for n in range(NT):
             in_copy(n).wait()
+        weights_start(0, NT)
         pl.semaphore_wait(barrier, group_size - 1)
         for n in range(NT):
             def in_stats(j, carry):
@@ -300,7 +308,7 @@
         pltpu.VMEM((4, NT, 2 * FR, 256), BF),
         pltpu.VMEM((NT, 2 * FR, 256), F32),
         pltpu.VMEM((4, 2 * FR, C), BF),
-        pltpu.VMEM((6, group_size, 8, C), F32),
+        pltpu.VMEM((6, group_size, 2, C), F32),
         pltpu.VMEM((8, C), F32),
         pltpu.SemaphoreType.DMA((RING, 3)),
         pltpu.SemaphoreType.DMA,
@@ -327,9 +335,9 @@
             body,
             out_shape=jax.ShapeDtypeStruct((frames * height * width, channels), BF),
             in_specs=[hbm, hbm, vmem, vmem, vmem, hbm, vmem],
-            out_specs=hbm,
+            out_specs=pl.BlockSpec(memory_space=pl.ANY),
             scratch_shapes=scratch,
-            compiler_params=pltpu.CompilerParams(collective_id=0, has_side_effects=True, vmem_limit_bytes=60 * 1024 * 1024),
+            compiler_params=pltpu.CompilerParams(collective_id=0, has_side_effects=True, vmem_limit_bytes=52 * 1024 * 1024),
             name="mid_block",
         )(latent.reshape(frames * height * width, channels), conv_w, conv_b, norm_g, norm_b, attn_w, attn_b)
         return out.reshape(latent.shape)

time: 125 us -> 117 us (0.936)
  Pallas kernels: 122 us -> 113 us
  local copies, waits for them, and re-layouts: 2.36 us -> 3.9 us
    pallas_call x1, Pallas kernels: 122 us -> 113 us  [device_body(): pl.pallas_call(body, out_shape=jax.ShapeDtypeStruct((frames * height * wi...]
    unnamed x1 -> x9, local copies, waits for them, and re-layouts: 2.36 us -> 3.9 us
where the time goes in v4:
time: 117 us
  Pallas kernels  113 us (97%)
  local copies, waits for them, and re-layouts  3.9 us (3%)
    pallas_call x1, Pallas kernels, device_body(): pl.pallas_call(body, out_shape=jax.ShapeDtypeStruct((frames * height * wi...  113 us
    unnamed x9, local copies, waits for them, and re-layouts  3.9 us

profile of v4, /device:TPU:0, one launch (start us, length us, event | category | flops | bytes accessed | tf_op | source)
XLA Modules:
  0.0 116.6 jit_solution(12207543416351636801)
XLA Ops:
  0.0 0.0 copy-start
  0.0 0.7 copy-done
  0.7 0.0 copy-start.1
  0.7 0.7 copy-done.1
  1.5 0.0 copy-start.2
  1.5 0.7 copy-done.2
  2.2 0.0 copy-start.3
  2.2 0.7 copy-done.3
  2.9 112.7 %mid_block.1 = bf16[768,768]{1,0:T(8,128)(2,1)S(1)} custom-call(bf16[768,768]{1,0:T(8,128)(2,1)} %bitcast.3, bf16[4,3,3,3,768,768]{5,4,3,2,1,0:T(8,128)(2,1)} %conv_w.1, f32[4,768]{1,0:T(4,128)S(1)} %copy-done.2, f32[5,768]{1,0:T(8,128)S(1)} %copy-done, f32[5,768]{1,0:T(8,128)S(1)} %copy-done.1, bf16[4,768,768]{2,1,0:T(8,128)(2,1)} %attn_w.1, ...), custom_call_target="tpu_custom_call" | custom-call | tf_op jit(solution)/shard_map/mid_block/pallas_call | solution.py:334
  115.6 1.0 copy.9
Async XLA Ops:
  0.0 0.7 copy-start
  0.7 0.7 copy-start.1
  1.5 0.7 copy-start.2
  2.2 0.7 copy-start.3

commit v5 on v4

--- a/solution.py
+++ b/solution.py
@@ -22,9 +22,9 @@
     units_conv = 3 * NT
     units_all = 4 * units_conv
 
-    def body(latent, conv_w, conv_b, norm_g, norm_b, attn_w, attn_b, out,
-             wbuf, awbuf, xs0, xs1, xs2, xs3, buf, halo, acc, qkv, stat, norm,
-             wsem, awsem, insem, outsem, hsend, hrecv, ssend, srecv):
+    def body(latent, conv_w, conv_b_in, norm_g_in, norm_b_in, attn_w, attn_b_in, out,
+             conv_b, norm_g, norm_b, attn_b, wbuf, awbuf, xs0, xs1, xs2, xs3, buf, halo, acc, qkv, stat, norm,
+             psem, wsem, awsem, insem, outsem, hsend, hrecv, ssend, srecv):
         me = lax.axis_index("time")
         xs = (xs0, xs1, xs2, xs3)
         xres = buf.at[0]
@@ -101,8 +101,12 @@
                 for w in weight_copies(u):
                     w.start()
 
+        small = [pltpu.make_async_copy(a, b, psem.at[i]) for i, (a, b) in enumerate(
+            ((conv_b_in, conv_b), (norm_g_in, norm_g), (norm_b_in, norm_b), (attn_b_in, attn_b)))]
         for n in range(NT):
             in_copy(n).start()
+        for p in small:
+            p.start()
 
         barrier = pltpu.get_barrier_semaphore()
         for p in range(1, group_size):
@@ -243,19 +247,18 @@
                             w.start()
 
         def attention(g):
-            def rows_norm(j, carry):
-                at = pl.ds(pl.multiple_of(j * width, width), width)
-                for k in range(NT):
+            attn_weight_copy().wait()
+            for k in range(NT):
+                for j in range(2 * height):
+                    at = slice(j * width, (j + 1) * width)
                     qkv[3, at, k * 256:(k + 1) * 256] = normed(xres[k, at, :], k).astype(BF)
-                return carry
-
-            lax.fori_loop(0, 2 * height, rows_norm, 0)
-            attn_weight_copy().wait()
             for w in range(3):
                 for n in range(NT):
                     cols = slice(n * 256, (n + 1) * 256)
-                    v = jnp.dot(qkv[3], awbuf[w, :, cols], preferred_element_type=F32) + attn_b[w:w + 1, cols]
-                    qkv[w, :, cols] = v.astype(BF)
+                    for f in range(2):
+                        rows = slice(f * FR, (f + 1) * FR)
+                        v = jnp.dot(qkv[3, rows, :], awbuf[w, :, cols], preferred_element_type=F32) + attn_b[w:w + 1, cols]
+                        qkv[w, rows, cols] = v.astype(BF)
             for f in range(2):
                 rows = slice(f * FR, (f + 1) * FR)
                 scores = lax.dot_general(qkv[0, rows, :], qkv[1, rows, :], (((1,), (1,)), ((), ())), preferred_element_type=F32)
@@ -265,15 +268,23 @@
                 qkv[3, rows, :] = jnp.dot(probs, qkv[2, rows, :], preferred_element_type=F32).astype(BF)
             for n in range(NT):
                 cols = slice(n * 256, (n + 1) * 256)
-                h = (jnp.dot(qkv[3], awbuf[3, :, cols], preferred_element_type=F32) + attn_b[3:4, cols]).astype(BF)
-                h = (xres[n].astype(F32) + h.astype(F32)).astype(BF)
-                xres[n] = h
-                hf = h.astype(F32)
-                put_stats(g + 1, n, fold(hf), fold(hf * hf))
+                s1 = jnp.zeros((8, 256), F32)
+                s2 = jnp.zeros((8, 256), F32)
+                for f in range(2):
+                    rows = slice(f * FR, (f + 1) * FR)
+                    h = (jnp.dot(qkv[3, rows, :], awbuf[3, :, cols], preferred_element_type=F32) + attn_b[3:4, cols]).astype(BF)
+                    h = (xres[n, rows, :].astype(F32) + h.astype(F32)).astype(BF)
+                    xres[n, rows, :] = h
+                    hf = h.astype(F32)
+                    s1 = s1 + fold(hf)
+                    s2 = s2 + fold(hf * hf)
+                put_stats(g + 1, n, s1, s2)
 
         for n in range(NT):
             in_copy(n).wait()
         weights_start(0, NT)
+        for p in small:
+            p.wait()
         pl.semaphore_wait(barrier, group_size - 1)
         for n in range(NT):
             def in_stats(j, carry):
@@ -298,6 +309,10 @@
             out_copy(n).wait()
 
     scratch = [
+        pltpu.VMEM((4, C), F32),
+        pltpu.VMEM((5, C), F32),
+        pltpu.VMEM((5, C), F32),
+        pltpu.VMEM((4, C), F32),
         pltpu.VMEM((RING, 3, 3, C, 256), BF),
         pltpu.VMEM((4, C, C), BF),
         pltpu.VMEM((FR, 3 * C), BF),
@@ -310,6 +325,7 @@
         pltpu.VMEM((4, 2 * FR, C), BF),
         pltpu.VMEM((6, group_size, 2, C), F32),
         pltpu.VMEM((8, C), F32),
+        pltpu.SemaphoreType.DMA((4,)),
         pltpu.SemaphoreType.DMA((RING, 3)),
         pltpu.SemaphoreType.DMA,
         pltpu.SemaphoreType.DMA((NT,)),
@@ -329,17 +345,17 @@
     def device_body(latent, conv_w, conv_b, norm_g, norm_b, attn_w, attn_b):
         frames, height, width, channels = latent.shape
         body, scratch = make_kernel(group_size, height, width, channels)
+        pinned = [pltpu.with_memory_space_constraint(p, pltpu.HBM) for p in (conv_b, norm_g, norm_b, attn_b)]
         hbm = pl.BlockSpec(memory_space=pltpu.HBM)
-        vmem = pl.BlockSpec(memory_space=pltpu.VMEM)
         out = pl.pallas_call(
             body,
             out_shape=jax.ShapeDtypeStruct((frames * height * width, channels), BF),
-            in_specs=[hbm, hbm, vmem, vmem, vmem, hbm, vmem],
+            in_specs=[hbm] * 7,
             out_specs=pl.BlockSpec(memory_space=pl.ANY),
             scratch_shapes=scratch,
             compiler_params=pltpu.CompilerParams(collective_id=0, has_side_effects=True, vmem_limit_bytes=52 * 1024 * 1024),
             name="mid_block",
-        )(latent.reshape(frames * height * width, channels), conv_w, conv_b, norm_g, norm_b, attn_w, attn_b)
+        )(latent.reshape(frames * height * width, channels), conv_w, *pinned[:3], attn_w, pinned[3])
         return out.reshape(latent.shape)
 
     return jax.shard_map(device_body, mesh=mesh, in_specs=(video_spec, P(), P(), P(), P(), P(), P()), out_specs=video_spec, check_vma=False)

time: 117 us -> 115 us (0.983)
  local copies, waits for them, and re-layouts: 3.9 us -> 1.02 us
    unnamed x9 -> x1, local copies, waits for them, and re-layouts: 3.9 us -> 1.02 us
where the time goes in v5:
time: 115 us
  Pallas kernels  114 us (99%)
    pallas_call x1, Pallas kernels, device_body(): pl.pallas_call(body, out_shape=jax.ShapeDtypeStruct((frames * height * wi...  114 us

profile of v5, /device:TPU:0, one launch (start us, length us, event | category | flops | bytes accessed | tf_op | source)
XLA Modules:
  0.0 114.6 jit_solution(3134316674935181159)
XLA Ops:
  0.0 113.5 %mid_block.1 = bf16[768,768]{1,0:T(8,128)(2,1)S(1)} custom-call(bf16[768,768]{1,0:T(8,128)(2,1)} %bitcast.3, bf16[4,3,3,3,768,768]{5,4,3,2,1,0:T(8,128)(2,1)} %conv_w.1, f32[4,768]{1,0:T(4,128)} %conv_b_in.1, f32[5,768]{1,0:T(8,128)} %norm_g_in.1, f32[5,768]{1,0:T(8,128)} %norm_b_in.1, bf16[4,768,768]{2,1,0:T(8,128)(2,1)} %attn_w.1, f32[4,768]{1,0:T(4,128)} %attn_b_in.1), custom_call_target="tpu_custom_call" | custom-call | tf_op jit(solution)/shard_map/mid_block/pallas_call | solution.py:350
  113.6 1.0 copy.9

commit v6 on v5

--- a/solution.py
+++ b/solution.py
@@ -24,7 +24,7 @@
 
     def body(latent, conv_w, conv_b_in, norm_g_in, norm_b_in, attn_w, attn_b_in, out,
              conv_b, norm_g, norm_b, attn_b, wbuf, awbuf, xs0, xs1, xs2, xs3, buf, halo, acc, qkv, stat, norm,
-             psem, wsem, awsem, insem, outsem, hsend, hrecv, ssend, srecv):
+             psem, wsem, awsem, insem, hsend, hrecv, ssend, srecv):
         me = lax.axis_index("time")
         xs = (xs0, xs1, xs2, xs3)
         xres = buf.at[0]
@@ -44,9 +44,6 @@
 
         def in_copy(n):
             return pltpu.make_async_copy(latent.at[:, pl.ds(n * 256, 256)], xres.at[n], insem.at[n])
-
-        def out_copy(n):
-            return pltpu.make_async_copy(xres.at[n], out.at[:, pl.ds(n * 256, 256)], outsem.at[n])
 
         def halo_copy(conv, n, f):
             return pltpu.make_async_remote_copy(
@@ -173,17 +170,18 @@
                 xs[slot][rows, at + 512:at + 768] = jnp.where(row_id == width - 1, 0.0, pltpu.roll(z, width - 1, 0)).astype(BF)
 
         def trip(slot, tap_t, n):
-            for d in (1, 0, 2):
+            for d in ((1, 0, 2) if tap_t == 2 else (0, 2, 1)):
                 w = jnp.concatenate([wbuf[slot, d, e, k * 256:(k + 1) * 256, :] for k in range(NT) for e in range(3)], axis=0)
                 rows = FR if d == 1 else FR - width
                 lo, dst = {0: (0, width), 1: (0, 0), 2: (width, 0)}[d]
-                lhs = jnp.concatenate([xs[tap_t + f][lo:lo + rows, :] for f in range(2)], axis=0)
+                order = (0, 1) if tap_t == 2 else (1, 0)
+                lhs = jnp.concatenate([xs[tap_t + f][lo:lo + rows, :] for f in order], axis=0)
                 r = jnp.dot(lhs, w, preferred_element_type=F32)
                 if d == 1 and tap_t == 2:
                     acc[n] = r
                 else:
-                    for f in range(2):
-                        acc[n, f * FR + dst:f * FR + dst + rows, :] += r[f * rows:(f + 1) * rows]
+                    for at, f in enumerate(order):
+                        acc[n, f * FR + dst:f * FR + dst + rows, :] += r[at * rows:(at + 1) * rows]
 
         def epilogue(c, n, g):
             odd = lax.rem(c, 2)
@@ -196,6 +194,7 @@
                 h = (acc[n, rows, :] + bias).astype(BF).astype(F32)
                 h = (xres[n, rows, :].astype(F32) * keep + h).astype(BF)
                 buf[1 - odd, n, rows, :] = h
+                out[rows, n * 256:(n + 1) * 256] = h
                 hf = h.astype(F32)
                 s1 = s1 + fold(hf)
                 s2 = s2 + fold(hf * hf)
@@ -303,10 +302,6 @@
             return carry
 
         lax.fori_loop(0, 4, layer, 0)
-        for n in range(NT):
-            out_copy(n).start()
-        for n in range(NT):
-            out_copy(n).wait()
 
     scratch = [
         pltpu.VMEM((4, C), F32),
@@ -329,7 +324,6 @@
         pltpu.SemaphoreType.DMA((RING, 3)),
         pltpu.SemaphoreType.DMA,
         pltpu.SemaphoreType.DMA((NT,)),
-        pltpu.SemaphoreType.DMA((NT,)),
         pltpu.SemaphoreType.DMA((4, NT, 2)),
         pltpu.SemaphoreType.DMA((4, NT, 2)),
         pltpu.SemaphoreType.DMA((5, group_size)),
@@ -351,7 +345,7 @@
             body,
             out_shape=jax.ShapeDtypeStruct((frames * height * width, channels), BF),
             in_specs=[hbm] * 7,
-            out_specs=pl.BlockSpec(memory_space=pl.ANY),
+            out_specs=pl.BlockSpec(memory_space=pltpu.VMEM),
             scratch_shapes=scratch,
             compiler_params=pltpu.CompilerParams(collective_id=0, has_side_effects=True, vmem_limit_bytes=52 * 1024 * 1024),
             name="mid_block",

time: 115 us -> 114 us (level)
  no operation moved by 1% of the time
where the time goes in v6:
time: 114 us
  Pallas kernels  113 us (99%)
    pallas_call x1, Pallas kernels, device_body(): pl.pallas_call(body, out_shape=jax.ShapeDtypeStruct((frames * height * wi...  113 us

profile of v6, /device:TPU:0, one launch (start us, length us, event | category | flops | bytes accessed | tf_op | source)
XLA Modules:
  0.0 114.0 jit_solution(7654359317636470767)
XLA Ops:
  0.0 113.0 %mid_block.1 = bf16[768,768]{1,0:T(8,128)(2,1)S(1)} custom-call(bf16[768,768]{1,0:T(8,128)(2,1)} %bitcast.3, bf16[4,3,3,3,768,768]{5,4,3,2,1,0:T(8,128)(2,1)} %conv_w.1, f32[4,768]{1,0:T(4,128)} %conv_b_in.1, f32[5,768]{1,0:T(8,128)} %norm_g_in.1, f32[5,768]{1,0:T(8,128)} %norm_b_in.1, bf16[4,768,768]{2,1,0:T(8,128)(2,1)} %attn_w.1, f32[4,768]{1,0:T(4,128)} %attn_b_in.1), custom_call_target="tpu_custom_call" | custom-call | tf_op jit(solution)/shard_map/mid_block/pallas_call | solution.py:344
  113.0 1.0 copy.9

commit v7 on v6

--- a/solution.py
+++ b/solution.py
@@ -205,11 +205,13 @@
             g_in = c + c // 2
             src = buf.at[lax.rem(c, 2)]
 
-            exchange(g_in, lambda: halo_start(c))
-
-            @pl.when(c == 0)
-            def _():
-                weights_start(NT, RING)
+            def behind_sums():
+                halo_start(c)
+                for n in range(NT):
+                    for w in weight_copies(base + NT + n):
+                        w.start()
+
+            exchange(g_in, behind_sums)
 
             for tap_t in (2, 1, 0):
                 first = base + (2 - tap_t) * NT
@@ -239,7 +241,7 @@
                     @pl.when(c == 0)
                     def _():
                         attn_weight_copy().start()
-                for n in range(NT):
+                for n in range(NT if tap_t > 0 else 0):
                     @pl.when(first + n + RING < units_all)
                     def _():
                         for w in weight_copies(first + n + RING):

time: 114 us -> 114 us (level)
  no operation moved by 1% of the time
where the time goes in v7:
time: 114 us
  Pallas kernels  113 us (99%)
    pallas_call x1, Pallas kernels, device_body(): pl.pallas_call(body, out_shape=jax.ShapeDtypeStruct((frames * height * wi...  113 us

profile of v7, /device:TPU:0, one launch (start us, length us, event | category | flops | bytes accessed | tf_op | source)
XLA Modules:
  0.0 113.8 jit_solution(10001282346428203414)
XLA Ops:
  0.0 112.8 %mid_block.1 = bf16[768,768]{1,0:T(8,128)(2,1)S(1)} custom-call(bf16[768,768]{1,0:T(8,128)(2,1)} %bitcast.3, bf16[4,3,3,3,768,768]{5,4,3,2,1,0:T(8,128)(2,1)} %conv_w.1, f32[4,768]{1,0:T(4,128)} %conv_b_in.1, f32[5,768]{1,0:T(8,128)} %norm_g_in.1, f32[5,768]{1,0:T(8,128)} %norm_b_in.1, bf16[4,768,768]{2,1,0:T(8,128)(2,1)} %attn_w.1, f32[4,768]{1,0:T(4,128)} %attn_b_in.1), custom_call_target="tpu_custom_call" | custom-call | tf_op jit(solution)/shard_map/mid_block/pallas_call | solution.py:346
  112.8 1.0 copy.9
